TPU v7x, 32 devices: a whole 2x2x4 slice. The times are simulated.
32 devices in a mesh: graph: 8 (over z, y), feat: 4 (over x, core).
Axes of the slice: x: 2, y: 2, z: 4, core: 2. Of those that a mesh axis runs over, the one named last changes fastest.
Arguments:
- node_feats: bfloat16 [2560, 512], P(('graph', 'feat')), may hold values from -6 to 6
- edge_feats: bfloat16 [16384, 512], P(('graph', 'feat')), may hold values from -6 to 6
- senders: int32 [16384], P(('graph', 'feat')), may hold values from 0 to 319
- receiver_ref: int32 [16384], P(('graph', 'feat')), may hold values from 0 to 1087, as said below
- send_list: int32 [8, 8, 96], P('graph'), may hold values from 0 to 319, as said below
- edge_count: int32 [8], P('graph'), may hold values from 1024 to 2048, as said below
- edge_w1: bfloat16 [1536, 512], replicated, may hold values from -0.15625 to 0.15625
- edge_w2: bfloat16 [512, 512], replicated, may hold values from -0.25 to 0.25
- edge_gain: bfloat16 [512], replicated, may hold values from 0.099609375 to 1.8984375
- edge_shift: bfloat16 [512], replicated, may hold values from -3 to 3
- node_w1: bfloat16 [1024, 512], replicated, may hold values from -0.1875 to 0.1875
- node_w2: bfloat16 [512, 512], replicated, may hold values from -0.25 to 0.25
- node_gain: bfloat16 [512], replicated, may hold values from 0.099609375 to 1.8984375
- node_shift: bfloat16 [512], replicated, may hold values from -3 to 3
Outputs:
- new_edges: bfloat16 [16384, 512], P(('graph', 'feat'))
- new_nodes: bfloat16 [2560, 512], P(('graph', 'feat'))
Inputs may be any that keep to these rules, and one draw needn't show every extreme that they name: `senders`: local node indices of the edge's own region. `receiver_ref`: A value below 320 is a node of the edge's own region. Otherwise q = value - 320 names slot q % 96 of the list that region s = q // 96 keeps for the edge's region; s is never the edge's own region, and when s is more than 2 steps away around the region order (either direction, wrapping) the slot is below 16. In every draw each region has an edge on slot 95 of the next region and an edge on slot 15 of the region 3 steps on. Each list send_list[s, g] holds 96 distinct local node indices of region s. Region g's live edges are its first edge_count[g] edge slots; some region has all 2048 live.
All inputs are finite; a program needn't handle non-finite values.
Results may differ from a plain program's by a relative error of at most 0.009.
Values may be sent and summed in bfloat16 or wider, within the bound.
A program may use at most 128 MiB of HBM per device.

v0:
```python
import jax
import jax.numpy as jnp
from jax import lax
from jax.sharding import PartitionSpec as P

NODE_DEV = 320
SLOT = 96
FAR_SLOT = 16
REACH = 2


epsilon = 1e-05


def passed_along(value, axis, by):
    devices = lax.axis_size(axis)
    return lax.ppermute(value, axis, [(i, (i + by) % devices) for i in range(devices)])


def layer_norm(outputs, norm_gain, norm_shift):
    average = jnp.mean(outputs, axis=-1, keepdims=True)
    centered = outputs - average
    variance = jnp.mean(centered * centered, axis=-1, keepdims=True)
    return centered * lax.rsqrt(variance + epsilon) * norm_gain + norm_shift


def perceptron(inputs, first_weight, second_weight, norm_gain, norm_shift):
    joined = jnp.concatenate(inputs, axis=1)
    activation = jnp.dot(joined, first_weight, preferred_element_type=jnp.float32)
    hidden = jax.nn.silu(activation).astype(jnp.bfloat16)
    outputs = jnp.dot(hidden, second_weight, preferred_element_type=jnp.float32)
    return layer_norm(outputs, norm_gain, norm_shift)


def one_hot_rows(indices, width):
    return (indices[:, None] == lax.iota(jnp.int32, width)[None, :]).astype(jnp.bfloat16)


def sum_into(selector, values):
    return lax.dot_general(
        selector, values, (((0,), (0,)), ((), ())), preferred_element_type=jnp.float32
    )


def per_device(
    node_feats,
    edge_feats,
    senders,
    receiver_ref,
    send_list,
    edge_count,
    edge_w1,
    edge_w2,
    edge_gain,
    edge_shift,
    node_w1,
    node_w2,
    node_gain,
    node_shift,
):
    feature_width = node_feats.shape[1]
    edge_local = edge_feats.shape[0]
    groups = lax.axis_size("graph")
    own_index = lax.axis_index("graph")
    share_index = lax.axis_index("feat")
    region_nodes = lax.all_gather(node_feats, "feat", axis=0, tiled=True)
    send_rows = send_list[0]
    pieces = 1
    part_index = 0
    quarter = SLOT // pieces
    far_count = FAR_SLOT // pieces
    my_rows = lax.dynamic_index_in_dim(
        send_rows.reshape(groups, quarter, pieces), part_index, 2, keepdims=False
    ).reshape(-1)
    list_select = one_hot_rows(my_rows, NODE_DEV)
    outgoing = (
        jnp.dot(list_select, region_nodes, preferred_element_type=jnp.float32)
        .astype(jnp.bfloat16)
        .reshape(groups, quarter, feature_width)
    )
    offsets = [distance for distance in range(-REACH, REACH + 1) if distance != 0]
    far_part = lax.all_to_all(
        outgoing[:, :far_count], "graph", split_axis=0, concat_axis=0, tiled=True
    )
    received = jnp.pad(far_part, ((0, 0), (0, quarter - far_count), (0, 0)))
    for distance in offsets:
        near_block = lax.dynamic_index_in_dim(
            outgoing, (own_index - distance) % groups, 0, keepdims=False
        )
        arrived = passed_along(near_block, "graph", -distance)
        received = lax.dynamic_update_index_in_dim(
            received, arrived, (own_index + distance) % groups, 0
        )
    offset = jnp.maximum(receiver_ref - NODE_DEV, 0)
    source = offset // SLOT
    slot_index = offset % SLOT
    arranged = source * SLOT + slot_index % pieces * quarter + slot_index // pieces
    row_index = jnp.where(receiver_ref < NODE_DEV, receiver_ref, NODE_DEV + arranged)
    table_rows = NODE_DEV + groups * SLOT
    table = jnp.concatenate([region_nodes, received.reshape(groups * SLOT, feature_width)], axis=0)
    receiver_select = one_hot_rows(row_index, table_rows)
    sender_select = one_hot_rows(senders, NODE_DEV)
    sender_rows = jnp.dot(sender_select, region_nodes, preferred_element_type=jnp.float32).astype(
        jnp.bfloat16
    )
    receiver_rows = jnp.dot(receiver_select, table, preferred_element_type=jnp.float32).astype(
        jnp.bfloat16
    )
    update = edge_feats.astype(jnp.float32) + perceptron(
        (edge_feats, sender_rows, receiver_rows), edge_w1, edge_w2, edge_gain, edge_shift
    )
    live_mask = share_index * edge_local + lax.iota(jnp.int32, edge_local) < edge_count[0]
    new_edges = jnp.where(live_mask[:, None], update, edge_feats.astype(jnp.float32)).astype(
        jnp.bfloat16
    )
    messages = jnp.where(live_mask[:, None], new_edges, jnp.zeros_like(new_edges))
    segment_totals = sum_into(receiver_select, messages)
    own_sums = segment_totals[:NODE_DEV]
    partial_value = segment_totals[NODE_DEV:].reshape(groups, SLOT, feature_width)
    far_back = lax.all_to_all(
        partial_value[:, :far_count].astype(jnp.bfloat16),
        "graph",
        split_axis=0,
        concat_axis=0,
        tiled=True,
    ).astype(jnp.float32)
    returned = jnp.pad(far_back, ((0, 0), (0, quarter - far_count), (0, 0)))
    for distance in offsets:
        near_block = lax.dynamic_index_in_dim(
            partial_value, (own_index + distance) % groups, 0, keepdims=False
        )
        arrived = passed_along(near_block.astype(jnp.bfloat16), "graph", distance).astype(
            near_block.dtype
        )
        returned = lax.dynamic_update_index_in_dim(
            returned, arrived, (own_index - distance) % groups, 0
        )
    flat_returned = returned.reshape(groups * quarter, feature_width)
    upper_part = flat_returned.astype(jnp.bfloat16)
    lower_part = (flat_returned - upper_part.astype(jnp.float32)).astype(jnp.bfloat16)
    listed_sums = sum_into(list_select, upper_part) + sum_into(list_select, lower_part)
    node_sums = lax.psum_scatter(
        (own_sums + listed_sums).astype(jnp.bfloat16), "feat", scatter_dimension=0, tiled=True
    )
    node_update = node_feats.astype(jnp.float32) + perceptron(
        (node_feats, node_sums), node_w1, node_w2, node_gain, node_shift
    )
    return (new_edges, node_update.astype(jnp.bfloat16))


def solution(mesh):
    return jax.shard_map(
        per_device,
        mesh=mesh,
        in_specs=(
            P(("graph", "feat"), None),
            P(("graph", "feat"), None),
            P(("graph", "feat")),
            P(("graph", "feat")),
            P("graph", None, None),
            P("graph"),
            P(),
            P(),
            P(),
            P(),
            P(),
            P(),
            P(),
            P(),
        ),
        out_specs=(P(("graph", "feat"), None), P(("graph", "feat"), None)),
        check_vma=False,
    )
```

profile of v0, /device:TPU:1, one launch (start us, length us, event | category | flops | bytes accessed | tf_op | source)
XLA Modules:
  0.0 91.7 jit_solution(2968659856400992377)
XLA Ops:
  7.3 7.8 %all_gather.3 = bf16[320,512]{1,0:T(8,128)(2,1)S(1)} all-gather(bf16[80,512]{1,0:T(8,128)(2,1)} %param.14), channel_id=1, replica_groups=mesh['graph'=8,'feat'=4] {'feat'}, dimensions={0}, use_global_device_ids=true | all-gather | bytes 409600 | tf_op jit(solution)/shard_map/all_gather | solution.py:66
  15.0 0.8 eq.67
  15.8 0.6 convolution_convert_fusion
  16.5 1.3 %collective-permute-start = (bf16[96,512]{1,0:T(8,128)(2,1)S(1)}, bf16[96,512]{1,0:T(8,128)(2,1)S(1)}, u32[]{:S(2)}, u32[]{:S(2)}) collective-permute-start(bf16[96,512]{1,0:T(8,128)(2,1)S(1)} %get-tuple-element.13), channel_id=1, source_target_pairs={{0,8},{4,12},{8,16},{12,20},{16,24},{20,28},{24,0},{28,4},{1,9},{5... | collective-permute-start | bytes 294920 | tf_op jit(solution)/shard_map/ppermute | solution.py:17
  17.8 0.7 slice.17
  18.5 4.5 %all-to-all-start = ((bf16[8,16,512]{2,1,0:T(8,128)(2,1)}), bf16[8,16,512]{2,1,0:T(8,128)(2,1)S(1)}, u32[]{:S(2)}, u32[]{:S(2)}) async-start(bf16[8,16,512]{2,1,0:T(8,128)(2,1)} %slice.17), calls=%async_computation | async-start | bytes 262144 | tf_op jit(solution)/shard_map/all_to_all | solution.py:82
  23.0 1.5 %collective-permute-start.1 = (bf16[96,512]{1,0:T(8,128)(2,1)S(1)}, bf16[96,512]{1,0:T(8,128)(2,1)S(1)}, u32[]{:S(2)}, u32[]{:S(2)}) collective-permute-start(bf16[96,512]{1,0:T(8,128)(2,1)S(1)} %get-tuple-element.12), channel_id=1, source_target_pairs={{0,4},{4,8},{8,12},{12,16},{16,20},{20,24},{24,28},{28,0},{1,5},{5... | collective-permute-start | bytes 294920 | tf_op jit(solution)/shard_map/ppermute | solution.py:17
  24.5 2.7 %collective-permute-start.2 = (bf16[96,512]{1,0:T(8,128)(2,1)S(1)}, bf16[96,512]{1,0:T(8,128)(2,1)S(1)}, u32[]{:S(2)}, u32[]{:S(2)}) collective-permute-start(bf16[96,512]{1,0:T(8,128)(2,1)S(1)} %get-tuple-element.11), channel_id=1, source_target_pairs={{0,28},{4,0},{8,4},{12,8},{16,12},{20,16},{24,20},{28,24},{1,29},{... | collective-permute-start | bytes 294920 | tf_op jit(solution)/shard_map/ppermute | solution.py:17
  27.2 1.4 %collective-permute-start.3 = (bf16[96,512]{1,0:T(8,128)(2,1)S(1)}, bf16[96,512]{1,0:T(8,128)(2,1)S(1)}, u32[]{:S(2)}, u32[]{:S(2)}) collective-permute-start(bf16[96,512]{1,0:T(8,128)(2,1)S(1)} %get-tuple-element.10), channel_id=1, source_target_pairs={{0,24},{4,28},{8,0},{12,4},{16,8},{20,12},{24,16},{28,20},{1,25},{... | collective-permute-start | bytes 294920 | tf_op jit(solution)/shard_map/ppermute | solution.py:17
  28.7 1.3 %convolution_convert_fusion.1 = bf16[512,512]{1,0:T(8,128)(2,1)} fusion(bf16[320,512]{1,0:T(8,128)(2,1)S(1)} %all_gather.3, s32[512]{0:T(512)S(1)} %copy-done.11), kind=kOutput, calls=%fused_computation.15 | convolution fusion | flops 168198144 | bytes 854016 | tf_op jit(solution)/shard_map/dot_general | solution.py:103
  30.6 1.0 %copy.16 = bf16[512,512]{0,1:T(8,128)(2,1)} copy(bf16[512,512]{1,0:T(8,128)(2,1)S(1)} %copy-done.2) | data formatting | bytes 1048576 | tf_op args[1]
  31.9 0.3 collective-permute-done.3
  32.2 1.7 %fusion.9 = bf16[512,512]{1,0:T(8,128)(2,1)} fusion(s32[512]{0:T(512)S(1)} %compare_select_fusion, bf16[768,512]{1,0:T(8,128)(2,1)S(1)} %bitcast.57, bf16[320,512]{1,0:T(8,128)(2,1)S(1)} %all_gather.3), kind=kOutput, calls=%fused_computation.14 | convolution fusion | flops 573472768 | bytes 1640448 | tf_op jit(solution)/shard_map/dot_general | solution.py:106
  34.0 2.9 %fusion.61 = (f32[512]{0:T(512)S(1)}, f32[512,512]{0,1:T(8,128)S(1)}) fusion(bf16[512,512]{1,0:T(8,128)(2,1)} %param.21, bf16[1536,512]{1,0:T(8,128)(2,1)S(1)} %copy-done, bf16[512,512]{1,0:T(8,128)(2,1)} %fusion.9, bf16[512,512]{1,0:T(8,128)(2,1)} %convolution_convert_fusion.1, bf16[512,512]{1,0:T(8,128)(2,1)S(1)} %copy-done.3), kind=kOutput, calls=%fused_computation.92 | convolution fusion | flops 1080032768 | bytes 4720640 | tf_op jit(solution)/shard_map/dot_general | solution.py:31
  37.0 1.4 %fusion.20 = bf16[512,512]{0,1:T(8,128)(2,1)S(1)} fusion(bf16[512,512]{0,1:T(8,128)(2,1)} %copy.16, f32[512,512]{0,1:T(8,128)S(1)} %get-tuple-element.15, f32[512]{0:T(512)S(1)} %convert_element_type.95, f32[512]{0:T(512)S(1)} %convert_element_type.94, f32[512]{0:T(512)S(1)} %add_rsqrt_fusion, f32[512]{0:T(512)S(1)} %broadcast_multiply_fusion, ...), kind=kLoop, calls=%fused_computation.27 | loop fusion | flops 2097152 | bytes 2105856 | tf_op jit(solution)/shard_map/convert_element_type | solution.py:113
  38.4 1.0 %fusion.12 = f32[1088,512]{1,0:T(8,128)S(1)} fusion(s32[512]{0:T(512)S(1)} %compare_select_fusion, bf16[512,512]{0,1:T(8,128)(2,1)S(1)} %fusion.20, pred[512]{0:T(512)(128)(4,1)S(1)} %add_compare_fusion), kind=kOutput, calls=%fused_computation.19 | convolution fusion | flops 571801600 | bytes 2755072 | tf_op jit(solution)/shard_map/dot_general | solution.py:40
  39.4 1.4 %copy-done.1 = f32[1088,512]{1,0:T(8,128)} copy-done((f32[1088,512]{1,0:T(8,128)}, f32[1088,512]{1,0:T(8,128)S(1)}, u32[]{:S(2)}) %copy-start.1) | copy-done | bytes 2228248
  40.9 0.7 slice.23
  41.5 4.0 %all-to-all-start.1 = ((bf16[8,16,512]{2,1,0:T(8,128)(2,1)}), bf16[8,16,512]{2,1,0:T(8,128)(2,1)S(1)}, u32[]{:S(2)}, u32[]{:S(2)}) async-start(bf16[8,16,512]{2,1,0:T(8,128)(2,1)} %slice.23), calls=%async_computation.1 | async-start | bytes 262144 | tf_op jit(solution)/shard_map/all_to_all | solution.py:120
  45.7 3.3 %collective-permute-start.4 = (bf16[96,512]{1,0:T(8,128)(2,1)S(1)}, bf16[96,512]{1,0:T(8,128)(2,1)S(1)}, u32[]{:S(2)}, u32[]{:S(2)}) collective-permute-start(bf16[96,512]{1,0:T(8,128)(2,1)S(1)} %get-tuple-element.9), channel_id=1, source_target_pairs={{0,24},{4,28},{8,0},{12,4},{16,8},{20,12},{24,16},{28,20},{1,25},{... | collective-permute-start | bytes 294920 | tf_op jit(solution)/shard_map/ppermute | solution.py:17
  48.9 1.2 %collective-permute-start.5 = (bf16[96,512]{1,0:T(8,128)(2,1)S(1)}, bf16[96,512]{1,0:T(8,128)(2,1)S(1)}, u32[]{:S(2)}, u32[]{:S(2)}) collective-permute-start(bf16[96,512]{1,0:T(8,128)(2,1)S(1)} %get-tuple-element.8), channel_id=1, source_target_pairs={{0,28},{4,0},{8,4},{12,8},{16,12},{20,16},{24,20},{28,24},{1,29},{... | collective-permute-start | bytes 294920 | tf_op jit(solution)/shard_map/ppermute | solution.py:17
  50.1 0.3 collective-permute-start.6
  50.4 0.9 collective-permute-start.7
  51.3 0.6 all-to-all-done.1
  52.1 1.1 %collective-permute-done.5 = bf16[96,512]{1,0:T(8,128)(2,1)S(1)} collective-permute-done((bf16[96,512]{1,0:T(8,128)(2,1)S(1)}, bf16[96,512]{1,0:T(8,128)(2,1)S(1)}, u32[]{:S(2)}, u32[]{:S(2)}) %collective-permute-start.5) | collective-permute-done | bytes 98336 | tf_op jit(solution)/shard_map/ppermute | solution.py:17
  53.2 3.3 %collective-permute-done.6 = bf16[96,512]{1,0:T(8,128)(2,1)S(1)} collective-permute-done((bf16[96,512]{1,0:T(8,128)(2,1)S(1)}, bf16[96,512]{1,0:T(8,128)(2,1)S(1)}, u32[]{:S(2)}, u32[]{:S(2)}) %collective-permute-start.6) | collective-permute-done | bytes 98336 | tf_op jit(solution)/shard_map/ppermute | solution.py:17
  56.9 0.7 fusion.14
  57.7 2.6 %fusion.11 = bf16[320,512]{1,0:T(8,128)(2,1)} fusion(f32[320,512]{1,0:T(8,128)S(1)} %fusion.14, bf16[768,512]{1,0:T(8,128)(2,1)S(1)} %get-tuple-element.5, f32[1088,512]{1,0:T(8,128)} %copy-done.1, s32[768]{0:T(1024)S(1)} %eq.67), kind=kOutput, calls=%fused_computation.18 | convolution fusion | flops 252395520 | bytes 2427904 | tf_op jit(solution)/shard_map/dot_general | solution.py:40
  60.4 1.0 %copy.17 = bf16[512,512]{1,0:T(8,128)(2,1)} copy(bf16[512,512]{0,1:T(8,128)(2,1)S(1)} %fusion.20) | data formatting | bytes 1048576
  61.4 20.8 %reduce-scatter.2.cloned.1.call-done = bf16[80,512]{1,0:T(8,128)(2,1)} async-done(((bf16[320,512]{1,0:T(8,128)(2,1)}), bf16[80,512]{1,0:T(8,128)(2,1)}) %reduce-scatter.2.cloned.1.call-update) | async-done | bytes 81936 | tf_op jit(solution)/shard_map/reduce_scatter | solution.py:142
  82.2 1.7 %fusion.64 = (f32[80]{0:T(128)S(1)}, f32[80,512]{1,0:T(8,128)S(1)}) fusion(bf16[512,512]{1,0:T(8,128)(2,1)} %param.25, bf16[1024,512]{1,0:T(8,128)(2,1)S(1)} %copy-done.10, bf16[80,512]{1,0:T(8,128)(2,1)} %reduce-scatter.2.cloned.1.call-done, bf16[80,512]{1,0:T(8,128)(2,1)S(1)} %copy-done.4), kind=kOutput, calls=%fused_computation.93 | convolution fusion | flops 126402480 | bytes 1900864 | tf_op jit(solution)/shard_map/dot_general | solution.py:31
  84.1 0.8 add_convert_fusion
  (57 shorter events, 1.4 us)
Async XLA Ops:
  7.2 26.8 %copy-start = (bf16[1536,512]{1,0:T(8,128)(2,1)S(1)}, bf16[1536,512]{1,0:T(8,128)(2,1)}, u32[]{:S(2)}) copy-start(bf16[1536,512]{1,0:T(8,128)(2,1)} %param.20) | copy-start | bytes 4718596
  7.2 21.4 %copy-start.11 = (s32[512]{0:T(512)S(1)}, s32[512]{0:T(512)}, u32[]{:S(2)}) copy-start(s32[512]{0:T(512)} %param.16) | copy-start | bytes 6148
  15.8 14.8 %copy-start.2 = (bf16[512,512]{1,0:T(8,128)(2,1)S(1)}, bf16[512,512]{1,0:T(8,128)(2,1)}, u32[]{:S(2)}) copy-start(bf16[512,512]{1,0:T(8,128)(2,1)} %param.15) | copy-start | bytes 1572868
  16.4 15.2 %copy-start.6 = (bf16[512]{0:T(512)(128)(2,1)S(1)}, bf16[512]{0:T(512)(128)(2,1)}, u32[]{:S(2)}) copy-start(bf16[512]{0:T(512)(128)(2,1)} %param.22) | copy-start | bytes 3076
  16.4 15.2 %copy-start.7 = (bf16[512]{0:T(512)(128)(2,1)S(1)}, bf16[512]{0:T(512)(128)(2,1)}, u32[]{:S(2)}) copy-start(bf16[512]{0:T(512)(128)(2,1)} %param.23) | copy-start | bytes 3076
  16.4 15.2 %copy-start.5 = (s32[512]{0:T(512)S(1)}, s32[512]{0:T(512)}, u32[]{:S(2)}) copy-start(s32[512]{0:T(512)} %param.17) | copy-start | bytes 6148
  16.5 15.3 %collective-permute-start = (bf16[96,512]{1,0:T(8,128)(2,1)S(1)}, bf16[96,512]{1,0:T(8,128)(2,1)S(1)}, u32[]{:S(2)}, u32[]{:S(2)}) collective-permute-start(bf16[96,512]{1,0:T(8,128)(2,1)S(1)} %get-tuple-element.13), channel_id=1, source_target_pairs={{0,8},{4,12},{8,16},{12,20},{16,24},{20,28},{24,0},{28,4},{1,9},{5... | collective-permute-start | bytes 294920 | tf_op jit(solution)/shard_map/ppermute | solution.py:17
  18.5 13.2 %all-to-all-start = ((bf16[8,16,512]{2,1,0:T(8,128)(2,1)}), bf16[8,16,512]{2,1,0:T(8,128)(2,1)S(1)}, u32[]{:S(2)}, u32[]{:S(2)}) async-start(bf16[8,16,512]{2,1,0:T(8,128)(2,1)} %slice.17), calls=%async_computation | async-start | bytes 262144 | tf_op jit(solution)/shard_map/all_to_all | solution.py:82
  23.0 8.8 %collective-permute-start.1 = (bf16[96,512]{1,0:T(8,128)(2,1)S(1)}, bf16[96,512]{1,0:T(8,128)(2,1)S(1)}, u32[]{:S(2)}, u32[]{:S(2)}) collective-permute-start(bf16[96,512]{1,0:T(8,128)(2,1)S(1)} %get-tuple-element.12), channel_id=1, source_target_pairs={{0,4},{4,8},{8,12},{12,16},{16,20},{20,24},{24,28},{28,0},{1,5},{5... | collective-permute-start | bytes 294920 | tf_op jit(solution)/shard_map/ppermute | solution.py:17
  24.5 7.3 %collective-permute-start.2 = (bf16[96,512]{1,0:T(8,128)(2,1)S(1)}, bf16[96,512]{1,0:T(8,128)(2,1)S(1)}, u32[]{:S(2)}, u32[]{:S(2)}) collective-permute-start(bf16[96,512]{1,0:T(8,128)(2,1)S(1)} %get-tuple-element.11), channel_id=1, source_target_pairs={{0,28},{4,0},{8,4},{12,8},{16,12},{20,16},{24,20},{28,24},{1,29},{... | collective-permute-start | bytes 294920 | tf_op jit(solution)/shard_map/ppermute | solution.py:17
  27.2 5.0 %collective-permute-start.3 = (bf16[96,512]{1,0:T(8,128)(2,1)S(1)}, bf16[96,512]{1,0:T(8,128)(2,1)S(1)}, u32[]{:S(2)}, u32[]{:S(2)}) collective-permute-start(bf16[96,512]{1,0:T(8,128)(2,1)S(1)} %get-tuple-element.10), channel_id=1, source_target_pairs={{0,24},{4,28},{8,0},{12,4},{16,8},{20,12},{24,16},{28,20},{1,25},{... | collective-permute-start | bytes 294920 | tf_op jit(solution)/shard_map/ppermute | solution.py:17
  32.2 1.7 %copy-start.3 = (bf16[512,512]{1,0:T(8,128)(2,1)S(1)}, bf16[512,512]{1,0:T(8,128)(2,1)}, u32[]{:S(2)}) copy-start(bf16[512,512]{1,0:T(8,128)(2,1)} %param.15) | copy-start | bytes 1572868
  39.4 1.4 %copy-start.1 = (f32[1088,512]{1,0:T(8,128)}, f32[1088,512]{1,0:T(8,128)S(1)}, u32[]{:S(2)}) copy-start(f32[1088,512]{1,0:T(8,128)S(1)} %fusion.12) | copy-start | bytes 6684676
  41.5 10.3 %all-to-all-start.1 = ((bf16[8,16,512]{2,1,0:T(8,128)(2,1)}), bf16[8,16,512]{2,1,0:T(8,128)(2,1)S(1)}, u32[]{:S(2)}, u32[]{:S(2)}) async-start(bf16[8,16,512]{2,1,0:T(8,128)(2,1)} %slice.23), calls=%async_computation.1 | async-start | bytes 262144 | tf_op jit(solution)/shard_map/all_to_all | solution.py:120
  45.6 36.6 %reduce-scatter.2.cloned.1.call-start = ((), (), s32[]{:S(2)}) async-start(), calls=%async_computation.3 | async-start | bytes 409600 | tf_op jit(solution)/shard_map/reduce_scatter | solution.py:142
  45.7 6.4 %collective-permute-start.4 = (bf16[96,512]{1,0:T(8,128)(2,1)S(1)}, bf16[96,512]{1,0:T(8,128)(2,1)S(1)}, u32[]{:S(2)}, u32[]{:S(2)}) collective-permute-start(bf16[96,512]{1,0:T(8,128)(2,1)S(1)} %get-tuple-element.9), channel_id=1, source_target_pairs={{0,24},{4,28},{8,0},{12,4},{16,8},{20,12},{24,16},{28,20},{1,25},{... | collective-permute-start | bytes 294920 | tf_op jit(solution)/shard_map/ppermute | solution.py:17
  48.9 4.3 %collective-permute-start.5 = (bf16[96,512]{1,0:T(8,128)(2,1)S(1)}, bf16[96,512]{1,0:T(8,128)(2,1)S(1)}, u32[]{:S(2)}, u32[]{:S(2)}) collective-permute-start(bf16[96,512]{1,0:T(8,128)(2,1)S(1)} %get-tuple-element.8), channel_id=1, source_target_pairs={{0,28},{4,0},{8,4},{12,8},{16,12},{20,16},{24,20},{28,24},{1,29},{... | collective-permute-start | bytes 294920 | tf_op jit(solution)/shard_map/ppermute | solution.py:17
  50.1 6.4 %collective-permute-start.6 = (bf16[96,512]{1,0:T(8,128)(2,1)S(1)}, bf16[96,512]{1,0:T(8,128)(2,1)S(1)}, u32[]{:S(2)}, u32[]{:S(2)}) collective-permute-start(bf16[96,512]{1,0:T(8,128)(2,1)S(1)} %get-tuple-element.7), channel_id=1, source_target_pairs={{0,4},{4,8},{8,12},{12,16},{16,20},{20,24},{24,28},{28,0},{1,5},{5... | collective-permute-start | bytes 294920 | tf_op jit(solution)/shard_map/ppermute | solution.py:17
  50.4 6.3 %collective-permute-start.7 = (bf16[96,512]{1,0:T(8,128)(2,1)S(1)}, bf16[96,512]{1,0:T(8,128)(2,1)S(1)}, u32[]{:S(2)}, u32[]{:S(2)}) collective-permute-start(bf16[96,512]{1,0:T(8,128)(2,1)S(1)} %get-tuple-element.6), channel_id=1, source_target_pairs={{0,8},{4,12},{8,16},{12,20},{16,24},{20,28},{24,0},{28,4},{1,9},{5... | collective-permute-start | bytes 294920 | tf_op jit(solution)/shard_map/ppermute | solution.py:17
  57.6 2.7 %copy-start.8 = (bf16[512]{0:T(512)(128)(2,1)S(1)}, bf16[512]{0:T(512)(128)(2,1)}, u32[]{:S(2)}) copy-start(bf16[512]{0:T(512)(128)(2,1)} %param.26) | copy-start | bytes 3076
  57.6 2.7 %copy-start.9 = (bf16[512]{0:T(512)(128)(2,1)S(1)}, bf16[512]{0:T(512)(128)(2,1)}, u32[]{:S(2)}) copy-start(bf16[512]{0:T(512)(128)(2,1)} %param.27) | copy-start | bytes 3076
  57.6 24.6 %copy-start.4 = (bf16[80,512]{1,0:T(8,128)(2,1)S(1)}, bf16[80,512]{1,0:T(8,128)(2,1)}, u32[]{:S(2)}) copy-start(bf16[80,512]{1,0:T(8,128)(2,1)} %param.14) | copy-start | bytes 245764
  57.6 24.5 %copy-start.10 = (bf16[1024,512]{1,0:T(8,128)(2,1)S(1)}, bf16[1024,512]{1,0:T(8,128)(2,1)}, u32[]{:S(2)}) copy-start(bf16[1024,512]{1,0:T(8,128)(2,1)} %param.24) | copy-start | bytes 3145732
Sparse Core Ops, SparseCore 0:
  60.4 21.7 reduce-scatter.1
where the time goes:
time: 93 us; the launch traced here: 91.7 us
  waiting for transfers between devices  26.4 us (28%)
  starting transfers between devices  21.2 us (23%)
  between operations  15.1 us (16%)
  matrix products  12.5 us (13%)
  blocking collectives  7.77 us (8%)
  local copies, waits for them, and re-layouts  5.82 us (6%)
  other arithmetic  2.93 us (3%)
    reduce_scatter x1, waiting for transfers between devices, per_device(): lax.psum_scatter((own_sums + listed_sums).astype(jnp.bfloat16), 'feat', s...  20.8 us
    ppermute x8, starting transfers between devices, passed_along(): lax.ppermute(value, axis, [(i, (i + by) % devices) for i in range(devices)])  12.6 us
    all_gather x1, blocking collectives, per_device(): region_nodes = lax.all_gather(node_feats, 'feat', axis=0, tiled=True)  7.77 us
    ppermute x8, waiting for transfers between devices, passed_along(): lax.ppermute(value, axis, [(i, (i + by) % devices) for i in range(devices)])  4.92 us
    dot_general x2, matrix products, perceptron(): outputs = jnp.dot(hidden, second_weight, preferred_element_type=jnp.float32)  4.57 us
    all_to_all x1, starting transfers between devices, per_device(): lax.all_to_all(outgoing[:, :far_count], 'graph', split_axis=0, concat_axi...  4.54 us
    dot_general x3, matrix products, sum_into(): lax.dot_general(selector, values, (((0,), (0,)), ((), ())), preferred_ele...  4.33 us
    all_to_all x1, starting transfers between devices, per_device(): lax.all_to_all(partial_value[:, :far_count].astype(jnp.bfloat16), 'graph'...  4.04 us
  transfers between devices with their start and end apart: 11, of which 6 were waited for; matrix products, arithmetic and copies ran while one was open for 5% of the time, Pallas kernels for 0%

commit v1 on v0

v1 whole, which is shorter than its diff:
```python
import functools

import jax
import jax.numpy as jnp
from jax import lax
from jax.experimental import pallas as pl
from jax.experimental.pallas import tpu as pltpu
from jax.sharding import PartitionSpec as P

FAR_SLOT = 16
REACH = 2
EPSILON = 1e-05
MESH = pl.DeviceIdType.MESH
F32 = jnp.float32
BF16 = jnp.bfloat16


def dot(a, b):
    return jnp.dot(a, b, preferred_element_type=F32)


def iota(shape, dim):
    return lax.broadcasted_iota(jnp.int32, shape, dim)


def silu(v):
    half = 0.5 * v
    return half + half * jnp.tanh(half)


def layer_norm(y, gain, shift):
    width = y.shape[1]
    mean = jnp.sum(y, axis=1, keepdims=True) * (1.0 / width)
    c = y - mean
    var = jnp.sum(c * c, axis=1, keepdims=True) * (1.0 / width)
    return c * lax.rsqrt(var + EPSILON) * gain + shift


def kernel(
    groups, feats,
    count_ref, nf, send_ref, recv_ref, list_ref, eg, es, ng, ns,
    ef_hbm, w1_hbm, w2_hbm, n1_hbm, n2_hbm,
    new_edges_hbm, new_nodes_hbm,
    ef, w1, w2, n1, n2, tab, lst, part, pair, halo, ret, agg_out, cross, agg, pre, oute, outn,
    load_sem, store_sem,
    ag_s, ag_r, rel_s, rel_r, h_s, h_r, hr_s, hr_r, p_s, p_r, b_s, b_r, x_s, x_r, d_s, d_r,
):
    g = lax.axis_index("graph")
    f = lax.axis_index("feat")
    n_own = nf.shape[0]
    width = nf.shape[1]
    half = width // 2
    edges = ef_hbm.shape[0]
    slot = list_ref.shape[2]
    region = n_own * feats
    chips = feats // 2
    chip = f // 2
    h = lax.rem(f, 2)
    other = 1 - h
    partner = chip * 2 + other
    mine = pl.ds(pl.multiple_of(h * half, half), half)
    theirs = pl.ds(pl.multiple_of(other * half, half), half)
    near = [d for d in range(1, REACH + 1)] + [groups - d for d in range(REACH, 0, -1)]
    far = list(range(REACH + 1, groups - REACH))
    blocks = [(d, i * slot, slot) for i, d in enumerate(near)]
    blocks += [(d, len(near) * slot + i * FAR_SLOT, FAR_SLOT) for i, d in enumerate(far)]
    order = list(range(len(near), len(blocks))) + [1, 2, 0, 3]
    listed = len(near) * slot + len(far) * FAR_SLOT

    def to(graph, feat):
        return {"graph": graph, "feat": feat}

    barrier = pltpu.get_barrier_semaphore()
    for k in range(1, feats):
        pl.semaphore_signal(barrier, inc=1, device_id=to(g, lax.rem(f + k, feats)), device_id_type=MESH)
    for d in range(1, groups):
        pl.semaphore_signal(barrier, inc=1, device_id=to(lax.rem(g + d, groups), f), device_id_type=MESH)

    loads = [
        pltpu.make_async_copy(src, dst, load_sem.at[i])
        for i, (src, dst) in enumerate(((ef_hbm, ef), (w1_hbm, w1), (w2_hbm, w2), (n1_hbm, n1), (n2_hbm, n2)))
    ]
    for load in loads:
        load.start()

    own_rows = pl.ds(pl.multiple_of(f * n_own, n_own), n_own)
    tab[own_rows, :] = nf[...]

    rr = recv_ref[...]
    offset = jnp.maximum(rr - region, 0)
    source = jnp.floor((offset.astype(F32) + 0.5) * (1.0 / slot)).astype(jnp.int32)
    slot_index = offset - source * slot
    dist = source - g
    dist = jnp.where(dist < 0, dist + groups, dist)
    base = len(near) * slot + (dist - REACH - 1) * FAR_SLOT
    for i, d in enumerate(near):
        base = jnp.where(dist == d, i * slot, base)
    row_index = jnp.where(rr < region, rr, region + base + slot_index)
    count = count_ref[0]
    live_lane = f * edges + iota((1, edges), 1) < count
    row_index = jnp.where(live_lane, row_index, -1)

    def down(index):
        wide = jnp.broadcast_to(index.astype(F32), (128, edges))
        return wide.T.astype(jnp.int32)

    def select(column, first, many):
        pieces = []
        for k in range(0, many, 128):
            w = min(128, many - k)
            pieces.append((column == iota((edges, 128), 1) + (first + k)).astype(F32).astype(BF16)[:, :w])
        return jnp.concatenate(pieces, axis=1) if len(pieces) > 1 else pieces[0]

    def list_rows(d, rows):
        index = list_ref[0, pl.ds(lax.rem(g + groups - d, groups), 1), :]
        return (iota((region, slot), 0) == index).astype(F32)[:, :rows]

    pl.semaphore_wait(barrier, feats - 1 + groups - 1)

    own_copy = pltpu.make_async_remote_copy(
        nf, tab.at[own_rows, :], ag_s.at[0], ag_r.at[0], device_id=to(g, partner), device_id_type=MESH)
    chip_copies = []
    for j in range(1, chips):
        for rel in range(2):
            hh = h if rel == 0 else other
            cols = mine if rel == 0 else theirs
            k = 1 + (j - 1) * 2 + rel
            chip_copies.append(pltpu.make_async_remote_copy(
                nf.at[:, cols], tab.at[own_rows, cols], ag_s.at[k], ag_r.at[k],
                device_id=to(g, lax.rem(chip + j, chips) * 2 + hh), device_id_type=MESH))
    for c in chip_copies:
        c.start()
    own_copy.start()

    loads[0].wait()
    loads[1].wait()
    pre[...] = dot(ef[...], w1[0:width, :])

    for c in chip_copies:
        c.wait_recv()
    own_copy.wait_recv()
    relays = []
    for j in range(1, chips):
        at = tab.at[pl.ds(pl.multiple_of(lax.rem(chip + chips - j, chips) * 2 * n_own, 2 * n_own), 2 * n_own), mine]
        relays.append(pltpu.make_async_remote_copy(
            at, at, rel_s.at[j - 1], rel_r.at[j - 1], device_id=to(g, partner), device_id_type=MESH))

    nodes_half = tab[0:region, mine]
    for i, (d, first, rows) in enumerate(blocks):
        lst[first:first + rows, :] = lax.dot_general(
            list_rows(d, rows).astype(BF16), nodes_half, (((0,), (0,)), ((), ())),
            preferred_element_type=F32).astype(BF16)
    halo_copies = {}
    for i in order:
        d, first, rows = blocks[i]
        halo_copies[i] = pltpu.make_async_remote_copy(
            lst.at[first:first + rows, :], halo.at[first:first + rows, mine], h_s.at[i], h_r.at[i],
            device_id=to(lax.rem(g + groups - d, groups), f), device_id_type=MESH)
        halo_copies[i].start()
    for c in relays:
        c.start()
    for c in relays:
        c.wait_recv()

    sender_sel = select(down(send_ref[...]), 0, region)
    column = down(row_index)
    pre[...] += dot(dot(sender_sel, tab[0:region, :]).astype(BF16), w1[width:2 * width, :])
    local_rows = dot(select(column, 0, region), tab[0:region, :]).astype(BF16)
    pre[...] += dot(local_rows, w1[2 * width:3 * width, :])

    share = {}
    for i in order:
        d, first, rows = blocks[i]
        halo_copies[i].wait_recv()
        at = halo.at[first:first + rows, mine]
        share[i] = pltpu.make_async_remote_copy(
            at, at, hr_s.at[i], hr_r.at[i], device_id=to(g, partner), device_id_type=MESH)
        share[i].start()
    for i in order:
        share[i].wait_recv()

    loads[2].wait()
    halo_sel = select(column, region, listed)
    table = halo[...]
    gain, shift = eg[...].astype(F32), es[...].astype(F32)
    step = edges // 2
    for k in range(0, edges, step):
        rows = slice(k, k + step)
        v = pre[rows, :] + dot(dot(halo_sel[rows, :], table).astype(BF16), w1[2 * width:3 * width, :])
        y = dot(silu(v).astype(BF16), w2[...])
        feats_in = ef[rows, :].astype(F32)
        update = feats_in + layer_norm(y, gain, shift)
        live = f * edges + k + iota((step, 1), 0) < count
        oute[rows, :] = jnp.where(live, update, feats_in).astype(BF16)

    edge_store = pltpu.make_async_copy(oute, new_edges_hbm, store_sem.at[0])
    edge_store.start()

    messages = oute[...]
    halo_selT = (iota((listed, edges), 0) + region == row_index).astype(F32).astype(BF16)
    part[0:listed, :] = dot(halo_selT, messages)
    pair_out = agg_out
    pair_out[0:listed, :] = part[0:listed, theirs].astype(BF16)
    first_pair = pltpu.make_async_remote_copy(
        pair_out.at[0:listed, :], pair.at[0:listed, :], p_s.at[0], p_r.at[0],
        device_id=to(g, partner), device_id_type=MESH)
    first_pair.start()
    own_selT = (iota((region, edges), 0) == row_index).astype(F32).astype(BF16)
    part[listed:listed + region, :] = dot(own_selT, messages)
    pair_out[listed:listed + region, :] = part[listed:listed + region, theirs].astype(BF16)
    second_pair = pltpu.make_async_remote_copy(
        pair_out.at[listed:listed + region, :], pair.at[listed:listed + region, :], p_s.at[1], p_r.at[1],
        device_id=to(g, partner), device_id_type=MESH)
    second_pair.start()

    first_pair.wait_recv()
    for c in halo_copies.values():
        c.wait_send()
    lst[...] = (part[0:listed, mine] + pair[0:listed, :].astype(F32)).astype(BF16)
    back = {}
    for i in order:
        d, first, rows = blocks[i]
        back[i] = pltpu.make_async_remote_copy(
            lst.at[first:first + rows, :], ret.at[first:first + rows, :], b_s.at[i], b_r.at[i],
            device_id=to(lax.rem(g + d, groups), f), device_id_type=MESH)
        back[i].start()

    loads[3].wait()
    loads[4].wait()
    node_in = nf[...]
    node_pre = dot(node_in, n1[0:width, :])
    second_pair.wait_recv()
    total = part[listed:listed + region, mine] + pair[listed:listed + region, :].astype(F32)
    for i in order:
        d, first, rows = blocks[i]
        back[i].wait_recv()
        total += dot(list_rows(d, rows).astype(BF16), ret[first:first + rows, :])
    part[0:region, 0:half] = total

    chip_rows = 2 * n_own
    for j in range(1, chips):
        at = pl.ds(pl.multiple_of(lax.rem(chip + j, chips) * chip_rows, chip_rows), chip_rows)
        cross[0, j - 1] = part[at, 0:half].astype(BF16)
    crosses = []
    for j in range(1, chips):
        crosses.append(pltpu.make_async_remote_copy(
            cross.at[0, j - 1], cross.at[1, j - 1], x_s.at[j - 1], x_r.at[j - 1],
            device_id=to(g, lax.rem(chip + j, chips) * 2 + h), device_id_type=MESH))
        crosses[-1].start()

    def chip_total(which):
        at = pl.ds(pl.multiple_of((chip * 2 + which) * n_own, n_own), n_own)
        rows = part[at, 0:half]
        local = pl.ds(pl.multiple_of(which * n_own, n_own), n_own)
        for j in range(1, chips):
            rows = rows + cross[1, j - 1, local, :].astype(F32)
        return rows.astype(BF16)

    for c in crosses:
        c.wait_recv()
    agg[0, :, 0:half] = chip_total(other)
    last = pltpu.make_async_remote_copy(
        agg.at[0, :, 0:half], agg.at[1, :, mine], d_s.at[0], d_r.at[0],
        device_id=to(g, partner), device_id_type=MESH)
    last.start()
    agg[1, :, mine] = chip_total(h)
    last.wait_recv()
    node_pre = node_pre + dot(agg[1], n1[width:2 * width, :])
    node_out = dot(silu(node_pre).astype(BF16), n2[...])
    outn[...] = (node_in.astype(F32) + layer_norm(node_out, ng[...].astype(F32), ns[...].astype(F32))).astype(BF16)
    node_store = pltpu.make_async_copy(outn, new_nodes_hbm, store_sem.at[1])
    node_store.start()

    own_copy.wait_send()
    for c in chip_copies + relays + list(share.values()) + [first_pair, second_pair]:
        c.wait_send()
    for c in list(back.values()) + crosses + [last]:
        c.wait_send()
    edge_store.wait()
    node_store.wait()


def per_device(node_feats, edge_feats, senders, receiver_ref, send_list, edge_count,
               edge_w1, edge_w2, edge_gain, edge_shift, node_w1, node_w2, node_gain, node_shift):
    groups = lax.axis_size("graph")
    feats = lax.axis_size("feat")
    n_own, width = node_feats.shape
    edges = edge_feats.shape[0]
    slot = send_list.shape[2]
    half = width // 2
    region = n_own * feats
    blocks = groups - 1
    listed = 2 * REACH * slot + (groups - 1 - 2 * REACH) * FAR_SLOT
    chips = feats // 2
    vmem = pl.BlockSpec(memory_space=pltpu.VMEM)
    hbm = pl.BlockSpec(memory_space=pl.ANY)
    smem = pl.BlockSpec(memory_space=pltpu.SMEM)
    dma = lambda n: pltpu.SemaphoreType.DMA((n,))
    links = 2 * max(chips - 1, 0) + 1
    return pl.pallas_call(
        functools.partial(kernel, groups, feats),
        out_shape=(jax.ShapeDtypeStruct((edges, width), BF16), jax.ShapeDtypeStruct((n_own, width), BF16)),
        in_specs=[smem] + [vmem] * 8 + [hbm] * 5,
        out_specs=(hbm, hbm),
        scratch_shapes=[
            pltpu.VMEM(edge_feats.shape, BF16), pltpu.VMEM(edge_w1.shape, BF16), pltpu.VMEM(edge_w2.shape, BF16),
            pltpu.VMEM(node_w1.shape, BF16), pltpu.VMEM(node_w2.shape, BF16),
            pltpu.VMEM((region, width), BF16),
            pltpu.VMEM((listed, half), BF16),
            pltpu.VMEM((listed + region, width), F32),
            pltpu.VMEM((listed + region, half), BF16),
            pltpu.VMEM((listed, width), BF16),
            pltpu.VMEM((listed, half), BF16),
            pltpu.VMEM((listed + region, half), BF16),
            pltpu.VMEM((2, chips - 1, 2 * n_own, half), BF16),
            pltpu.VMEM((2, n_own, width), BF16),
            pltpu.VMEM((edges, edge_w1.shape[1]), F32),
            pltpu.VMEM((edges, width), BF16),
            pltpu.VMEM((n_own, width), BF16),
            dma(5), dma(2),
            dma(links), dma(links), dma(chips - 1), dma(chips - 1),
            dma(blocks), dma(blocks), dma(blocks), dma(blocks),
            dma(2), dma(2), dma(blocks), dma(blocks), dma(chips - 1), dma(chips - 1), dma(1), dma(1),
        ],
        compiler_params=pltpu.CompilerParams(
            collective_id=0, has_side_effects=True, vmem_limit_bytes=60 * 1024 * 1024),
    )(edge_count, node_feats, senders.reshape(1, edges), receiver_ref.reshape(1, edges), send_list,
      edge_gain.reshape(1, width), edge_shift.reshape(1, width),
      node_gain.reshape(1, width), node_shift.reshape(1, width),
      edge_feats, edge_w1, edge_w2, node_w1, node_w2)


def solution(mesh):
    whole = P()
    rows = P(("graph", "feat"), None)
    flat = P(("graph", "feat"))
    return jax.shard_map(
        per_device,
        mesh=mesh,
        in_specs=(rows, rows, flat, flat, P("graph", None, None), P("graph")) + (whole,) * 8,
        out_specs=(rows, rows),
        check_vma=False,
    )
```

time: 93 us -> 45 us (0.48); the launches traced: 91.7 us -> 44.7 us
  Pallas kernels: 0 us -> 35 us
  waiting for transfers between devices: 26.4 us -> 0 us
  starting transfers between devices: 21.2 us -> 0 us
  between operations: 15.1 us -> 1.29 us
  matrix products: 12.5 us -> 0 us
  blocking collectives: 7.77 us -> 0 us
  other arithmetic: 2.93 us -> 0 us
  local copies, waits for them, and re-layouts: 5.82 us -> 8.44 us
    pallas_call x0 -> x1, Pallas kernels: none -> 35 us  [per_device(): pl.pallas_call(functools.partial(kernel, groups, feats), out_shape=(jax.S...]
    reduce_scatter x1 -> x0, waiting for transfers between devices: 20.8 us -> none  [per_device(): lax.psum_scatter((own_sums + listed_sums).astype(jnp.bfloat16), 'feat', s...]
    ppermute x8 -> x0, starting transfers between devices: 12.6 us -> none  [passed_along(): lax.ppermute(value, axis, [(i, (i + by) % devices) for i in range(devices)])]
    dot_general x8 -> x0, matrix products: 12.5 us -> none  [the longest x2 4.57 us: perceptron(): outputs = jnp.dot(hidden, second_weight, preferred_element_type=jnp.float32)]
    all_to_all x2 -> x0, starting transfers between devices: 8.58 us -> none  [the longest x1 4.54 us: per_device(): lax.all_to_all(outgoing[:, :far_count], 'graph', split_axis=0, concat_axi...]
    all_gather x1 -> x0, blocking collectives: 7.77 us -> none  [per_device(): region_nodes = lax.all_gather(node_feats, 'feat', axis=0, tiled=True)]
    reshape x0 -> x4, local copies, waits for them, and re-layouts: none -> 5.05 us  [the longest x1 1.27 us: per_device(): node_shift.reshape(1, width)]
    ppermute x8 -> x0, waiting for transfers between devices: 4.92 us -> none  [passed_along(): lax.ppermute(value, axis, [(i, (i + by) % devices) for i in range(devices)])]
  transfers between devices with their start and end apart: 11 -> 0, of which waited for: 6 -> 0; matrix products, arithmetic and copies ran while one was open for 5% -> 0% of each run, Pallas kernels for 0% -> 0%
where the time goes in v1:
time: 45 us; the launch traced here: 44.7 us
  Pallas kernels  35 us (78%)
  local copies, waits for them, and re-layouts  8.44 us (19%)
  between operations  1.29 us (3%)
    pallas_call x1, Pallas kernels, per_device(): pl.pallas_call(functools.partial(kernel, groups, feats), out_shape=(jax.S...  35 us
    unnamed x2, local copies, waits for them, and re-layouts  3.4 us
    reshape x1, local copies, waits for them, and re-layouts, per_device(): node_shift.reshape(1, width)  1.27 us
    reshape x1, local copies, waits for them, and re-layouts, per_device(): edge_gain.reshape(1, width)  1.26 us
    reshape x1, local copies, waits for them, and re-layouts, per_device(): node_gain.reshape(1, width)  1.26 us
    reshape x1, local copies, waits for them, and re-layouts, per_device(): edge_shift.reshape(1, width)  1.26 us

profile of v1, /device:TPU:1, one launch (start us, length us, event | category | flops | bytes accessed | tf_op | source)
XLA Modules:
  0.0 44.7 jit_solution(2088348107562142995)
XLA Ops:
  1.3 1.3 %reshape.24.eg = bf16[1,512]{1,0:T(2,128)(2,1)} reshape(bf16[512]{0:T(512)(128)(2,1)} %param.22) | data formatting | bytes 2048 | tf_op jit(solution)/shard_map/reshape | solution.py:328
  2.5 1.3 %reshape.25.es = bf16[1,512]{1,0:T(2,128)(2,1)} reshape(bf16[512]{0:T(512)(128)(2,1)} %param.23) | data formatting | bytes 2048 | tf_op jit(solution)/shard_map/reshape | solution.py:328
  3.8 1.3 %reshape.26.ng = bf16[1,512]{1,0:T(2,128)(2,1)} reshape(bf16[512]{0:T(512)(128)(2,1)} %param.26) | data formatting | bytes 2048 | tf_op jit(solution)/shard_map/reshape | solution.py:329
  5.1 1.3 %reshape.27.ns = bf16[1,512]{1,0:T(2,128)(2,1)} reshape(bf16[512]{0:T(512)(128)(2,1)} %param.27) | data formatting | bytes 2048 | tf_op jit(solution)/shard_map/reshape | solution.py:329
  6.3 35.0 %shard_map.149 = (bf16[512,512]{1,0:T(8,128)(2,1)}, bf16[80,512]{1,0:T(8,128)(2,1)}) custom-call(s32[1]{0:T(128)S(6)} %copy.18.count_ref, bf16[80,512]{1,0:T(8,128)(2,1)} %nf.1, s32[1,512]{1,0:T(1,128)} %bitcast.2, s32[1,512]{1,0:T(1,128)} %bitcast.3, s32[1,8,96]{2,1,0:T(8,128)} %list_ref.1, bf16[1,512]{1,0:T(2,128)(2,1)} %reshape.24.eg, ...), custom_call_target="tpu_custom_call" | custom-call | tf_op jit(solution)/shard_map/pallas_call | solution.py:300
  41.3 1.9 %copy.19 = bf16[512,512]{1,0:T(8,128)(2,1)} copy(bf16[512,512]{1,0:T(8,128)(2,1)} %get-tuple-element.4) | data formatting | bytes 1048576
  43.2 1.5 %copy.20 = bf16[80,512]{1,0:T(8,128)(2,1)} copy(bf16[80,512]{1,0:T(8,128)(2,1)} %get-tuple-element.5) | data formatting | bytes 163840

commit v2 on v1

--- a/solution.py
+++ b/solution.py
@@ -38,20 +38,20 @@
 
 def kernel(
     groups, feats,
+    count_hbm, nf_hbm, send_hbm, recv_hbm, list_hbm, eg_hbm, es_hbm, ng_hbm, ns_hbm,
+    ef_hbm, w1_hbm, w2_hbm, n1_hbm, n2_hbm,
+    oute, outn,
     count_ref, nf, send_ref, recv_ref, list_ref, eg, es, ng, ns,
-    ef_hbm, w1_hbm, w2_hbm, n1_hbm, n2_hbm,
-    new_edges_hbm, new_nodes_hbm,
-    ef, w1, w2, n1, n2, tab, lst, part, pair, halo, ret, agg_out, cross, agg, pre, oute, outn,
-    load_sem, store_sem,
+    ef, w1, w2, n1, n2, tab, lst, part, pair, halo, ret, agg_out, cross, agg, pre,
+    load_sem,
     ag_s, ag_r, rel_s, rel_r, h_s, h_r, hr_s, hr_r, p_s, p_r, b_s, b_r, x_s, x_r, d_s, d_r,
 ):
     g = lax.axis_index("graph")
     f = lax.axis_index("feat")
-    n_own = nf.shape[0]
-    width = nf.shape[1]
+    n_own, width = nf.shape
     half = width // 2
     edges = ef_hbm.shape[0]
-    slot = list_ref.shape[2]
+    slot = list_hbm.shape[2]
     region = n_own * feats
     chips = feats // 2
     chip = f // 2
@@ -78,10 +78,15 @@
 
     loads = [
         pltpu.make_async_copy(src, dst, load_sem.at[i])
-        for i, (src, dst) in enumerate(((ef_hbm, ef), (w1_hbm, w1), (w2_hbm, w2), (n1_hbm, n1), (n2_hbm, n2)))
+        for i, (src, dst) in enumerate((
+            (nf_hbm, nf), (recv_hbm, recv_ref), (send_hbm, send_ref), (count_hbm, count_ref), (list_hbm, list_ref),
+            (ef_hbm, ef), (w1_hbm, w1), (w2_hbm, w2), (eg_hbm, eg), (es_hbm, es),
+            (n1_hbm, n1), (n2_hbm, n2), (ng_hbm, ng), (ns_hbm, ns)))
     ]
     for load in loads:
         load.start()
+    for load in loads[:5]:
+        load.wait()
 
     own_rows = pl.ds(pl.multiple_of(f * n_own, n_own), n_own)
     tab[own_rows, :] = nf[...]
@@ -132,8 +137,8 @@
         c.start()
     own_copy.start()
 
-    loads[0].wait()
-    loads[1].wait()
+    loads[5].wait()
+    loads[6].wait()
     pre[...] = dot(ef[...], w1[0:width, :])
 
     for c in chip_copies:
@@ -179,10 +184,11 @@
     for i in order:
         share[i].wait_recv()
 
-    loads[2].wait()
+    for load in loads[7:10]:
+        load.wait()
     halo_sel = select(column, region, listed)
     table = halo[...]
-    gain, shift = eg[...].astype(F32), es[...].astype(F32)
+    gain, shift = eg[...].astype(F32).reshape(1, width), es[...].astype(F32).reshape(1, width)
     step = edges // 2
     for k in range(0, edges, step):
         rows = slice(k, k + step)
@@ -192,9 +198,6 @@
         update = feats_in + layer_norm(y, gain, shift)
         live = f * edges + k + iota((step, 1), 0) < count
         oute[rows, :] = jnp.where(live, update, feats_in).astype(BF16)
-
-    edge_store = pltpu.make_async_copy(oute, new_edges_hbm, store_sem.at[0])
-    edge_store.start()
 
     messages = oute[...]
     halo_selT = (iota((listed, edges), 0) + region == row_index).astype(F32).astype(BF16)
@@ -225,8 +228,8 @@
             device_id=to(lax.rem(g + d, groups), f), device_id_type=MESH)
         back[i].start()
 
-    loads[3].wait()
-    loads[4].wait()
+    for load in loads[10:14]:
+        load.wait()
     node_in = nf[...]
     node_pre = dot(node_in, n1[0:width, :])
     second_pair.wait_recv()
@@ -267,17 +270,13 @@
     last.wait_recv()
     node_pre = node_pre + dot(agg[1], n1[width:2 * width, :])
     node_out = dot(silu(node_pre).astype(BF16), n2[...])
-    outn[...] = (node_in.astype(F32) + layer_norm(node_out, ng[...].astype(F32), ns[...].astype(F32))).astype(BF16)
-    node_store = pltpu.make_async_copy(outn, new_nodes_hbm, store_sem.at[1])
-    node_store.start()
+    outn[...] = (node_in.astype(F32) + layer_norm(node_out, ng[...].astype(F32).reshape(1, width), ns[...].astype(F32).reshape(1, width))).astype(BF16)
 
     own_copy.wait_send()
     for c in chip_copies + relays + list(share.values()) + [first_pair, second_pair]:
         c.wait_send()
     for c in list(back.values()) + crosses + [last]:
         c.wait_send()
-    edge_store.wait()
-    node_store.wait()
 
 
 def per_device(node_feats, edge_feats, senders, receiver_ref, send_list, edge_count,
@@ -294,15 +293,17 @@
     chips = feats // 2
     vmem = pl.BlockSpec(memory_space=pltpu.VMEM)
     hbm = pl.BlockSpec(memory_space=pl.ANY)
-    smem = pl.BlockSpec(memory_space=pltpu.SMEM)
     dma = lambda n: pltpu.SemaphoreType.DMA((n,))
     links = 2 * max(chips - 1, 0) + 1
     return pl.pallas_call(
         functools.partial(kernel, groups, feats),
-        out_shape=(jax.ShapeDtypeStruct((edges, width), BF16), jax.ShapeDtypeStruct((n_own, width), BF16)),
-        in_specs=[smem] + [vmem] * 8 + [hbm] * 5,
-        out_specs=(hbm, hbm),
+        out_shape=(pltpu.VMEM((edges, width), BF16), pltpu.VMEM((n_own, width), BF16)),
+        in_specs=[hbm] * 14,
+        out_specs=(vmem, vmem),
         scratch_shapes=[
+            pltpu.SMEM(edge_count.shape, jnp.int32), pltpu.VMEM(node_feats.shape, BF16),
+            pltpu.VMEM((1, edges), jnp.int32), pltpu.VMEM((1, edges), jnp.int32), pltpu.VMEM(send_list.shape, jnp.int32),
+        ] + [pltpu.VMEM((width,), BF16)] * 4 + [
             pltpu.VMEM(edge_feats.shape, BF16), pltpu.VMEM(edge_w1.shape, BF16), pltpu.VMEM(edge_w2.shape, BF16),
             pltpu.VMEM(node_w1.shape, BF16), pltpu.VMEM(node_w2.shape, BF16),
             pltpu.VMEM((region, width), BF16),
@@ -315,9 +316,7 @@
             pltpu.VMEM((2, chips - 1, 2 * n_own, half), BF16),
             pltpu.VMEM((2, n_own, width), BF16),
             pltpu.VMEM((edges, edge_w1.shape[1]), F32),
-            pltpu.VMEM((edges, width), BF16),
-            pltpu.VMEM((n_own, width), BF16),
-            dma(5), dma(2),
+            dma(14),
             dma(links), dma(links), dma(chips - 1), dma(chips - 1),
             dma(blocks), dma(blocks), dma(blocks), dma(blocks),
             dma(2), dma(2), dma(blocks), dma(blocks), dma(chips - 1), dma(chips - 1), dma(1), dma(1),
@@ -325,8 +324,7 @@
         compiler_params=pltpu.CompilerParams(
             collective_id=0, has_side_effects=True, vmem_limit_bytes=60 * 1024 * 1024),
     )(edge_count, node_feats, senders.reshape(1, edges), receiver_ref.reshape(1, edges), send_list,
-      edge_gain.reshape(1, width), edge_shift.reshape(1, width),
-      node_gain.reshape(1, width), node_shift.reshape(1, width),
+      edge_gain, edge_shift, node_gain, node_shift,
       edge_feats, edge_w1, edge_w2, node_w1, node_w2)
 
 

time: 45 us -> 36.4 us (0.81)
  local copies, waits for them, and re-layouts: 8.44 us -> 1.43 us
  Pallas kernels: 35 us -> 33.5 us
    reshape x4 -> x0, local copies, waits for them, and re-layouts: 5.05 us -> none  [the longest x1 1.27 us: per_device(): node_shift.reshape(1, width)]
    unnamed x2, local copies, waits for them, and re-layouts: 3.4 us -> 1.43 us
    pallas_call x1, Pallas kernels: 35 us -> 33.5 us  [per_device(): pl.pallas_call(functools.partial(kernel, groups, feats), out_shape=(pltpu...]
where the time goes in v2:
time: 36.4 us; the launch traced here: 36.3 us
  Pallas kernels  33.5 us (92%)
  local copies, waits for them, and re-layouts  1.43 us (4%)
  between operations  1.29 us (4%)
    pallas_call x1, Pallas kernels, per_device(): pl.pallas_call(functools.partial(kernel, groups, feats), out_shape=(pltpu...  33.5 us
    unnamed x2, local copies, waits for them, and re-layouts  1.43 us

profile of v2, /device:TPU:1, one launch (start us, length us, event | category | flops | bytes accessed | tf_op | source)
XLA Modules:
  0.0 36.3 jit_solution(17878237331894357130)
XLA Ops:
  1.3 33.5 %shard_map.149 = (bf16[512,512]{1,0:T(8,128)(2,1)S(1)}, bf16[80,512]{1,0:T(8,128)(2,1)S(1)}) custom-call(s32[1]{0:T(128)S(6)} %copy.20.count_hbm, bf16[80,512]{1,0:T(8,128)(2,1)} %nf_hbm.1, s32[1,512]{1,0:T(1,128)} %bitcast.2, s32[1,512]{1,0:T(1,128)} %bitcast.3, s32[1,8,96]{2,1,0:T(8,128)} %list_hbm.1, bf16[512]{0:T(512)(128)(2,1)} %eg_hbm.1, ...), custom_call_target="tpu_custom_call" | custom-call | tf_op jit(solution)/shard_map/pallas_call | solution.py:298
  34.8 0.8 %copy.18 = bf16[512,512]{1,0:T(8,128)(2,1)} copy(bf16[512,512]{1,0:T(8,128)(2,1)S(1)} %get-tuple-element.2) | data formatting | bytes 1048576
  35.6 0.6 %copy.19 = bf16[80,512]{1,0:T(8,128)(2,1)} copy(bf16[80,512]{1,0:T(8,128)(2,1)S(1)} %get-tuple-element.3) | data formatting | bytes 163840

commit v3 on v2

--- a/solution.py
+++ b/solution.py
@@ -42,9 +42,10 @@
     ef_hbm, w1_hbm, w2_hbm, n1_hbm, n2_hbm,
     oute, outn,
     count_ref, nf, send_ref, recv_ref, list_ref, eg, es, ng, ns,
-    ef, w1, w2, n1, n2, tab, lst, part, pair, halo, ret, agg_out, cross, agg, pre,
+    ef, w1, w2, n1, n2, tab, lst, part, pair, halo, ret, pair_out, own16, sums, pre,
+    list_sel, list_selT, recv_sel, recv_selT,
     load_sem,
-    ag_s, ag_r, rel_s, rel_r, h_s, h_r, hr_s, hr_r, p_s, p_r, b_s, b_r, x_s, x_r, d_s, d_r,
+    ag_s, ag_r, rel_s, rel_r, h_s, h_r, hr_s, hr_r, p_s, p_r, b_s, b_r, x_s, x_r,
 ):
     g = lax.axis_index("graph")
     f = lax.axis_index("feat")
@@ -120,6 +121,14 @@
         index = list_ref[0, pl.ds(lax.rem(g + groups - d, groups), 1), :]
         return (iota((region, slot), 0) == index).astype(F32)[:, :rows]
 
+    for d, first, rows in blocks:
+        index = list_ref[0, pl.ds(lax.rem(g + groups - d, groups), 1), :].astype(F32)
+        wide = jnp.broadcast_to(index, (128, slot)).T[:rows, :]
+        for k in range(0, region, 128):
+            w = min(128, region - k)
+            hit = wide == (iota((rows, 128), 1) + k).astype(F32)
+            list_sel[first:first + rows, k:k + w] = hit.astype(F32).astype(BF16)[:, :w]
+
     pl.semaphore_wait(barrier, feats - 1 + groups - 1)
 
     own_copy = pltpu.make_async_remote_copy(
@@ -137,10 +146,6 @@
         c.start()
     own_copy.start()
 
-    loads[5].wait()
-    loads[6].wait()
-    pre[...] = dot(ef[...], w1[0:width, :])
-
     for c in chip_copies:
         c.wait_recv()
     own_copy.wait_recv()
@@ -150,11 +155,7 @@
         relays.append(pltpu.make_async_remote_copy(
             at, at, rel_s.at[j - 1], rel_r.at[j - 1], device_id=to(g, partner), device_id_type=MESH))
 
-    nodes_half = tab[0:region, mine]
-    for i, (d, first, rows) in enumerate(blocks):
-        lst[first:first + rows, :] = lax.dot_general(
-            list_rows(d, rows).astype(BF16), nodes_half, (((0,), (0,)), ((), ())),
-            preferred_element_type=F32).astype(BF16)
+    lst[...] = dot(list_sel[...], tab[0:region, mine]).astype(BF16)
     halo_copies = {}
     for i in order:
         d, first, rows = blocks[i]
@@ -164,14 +165,22 @@
         halo_copies[i].start()
     for c in relays:
         c.start()
+
+    sender_sel = select(down(send_ref[...]), 0, region)
+    column = down(row_index)
+    recv_sel[...] = select(column, 0, region + listed)
+    recv_selT[...] = (iota((region + listed, edges), 0) == row_index).astype(F32).astype(BF16)
+    for d, first, rows in blocks:
+        list_selT[:, first:first + rows] = list_rows(d, rows).astype(BF16)
+
     for c in relays:
         c.wait_recv()
-
-    sender_sel = select(down(send_ref[...]), 0, region)
-    column = down(row_index)
-    pre[...] += dot(dot(sender_sel, tab[0:region, :]).astype(BF16), w1[width:2 * width, :])
-    local_rows = dot(select(column, 0, region), tab[0:region, :]).astype(BF16)
-    pre[...] += dot(local_rows, w1[2 * width:3 * width, :])
+    loads[5].wait()
+    loads[6].wait()
+    pre[...] = (
+        dot(ef[...], w1[0:width, :])
+        + dot(dot(sender_sel, tab[0:region, :]).astype(BF16), w1[width:2 * width, :])
+        + dot(dot(recv_sel[:, 0:region], tab[0:region, :]).astype(BF16), w1[2 * width:3 * width, :]))
 
     share = {}
     for i in order:
@@ -186,40 +195,34 @@
 
     for load in loads[7:10]:
         load.wait()
-    halo_sel = select(column, region, listed)
     table = halo[...]
     gain, shift = eg[...].astype(F32).reshape(1, width), es[...].astype(F32).reshape(1, width)
     step = edges // 2
     for k in range(0, edges, step):
         rows = slice(k, k + step)
-        v = pre[rows, :] + dot(dot(halo_sel[rows, :], table).astype(BF16), w1[2 * width:3 * width, :])
+        v = pre[rows, :] + dot(dot(recv_sel[rows, region:region + listed], table).astype(BF16), w1[2 * width:3 * width, :])
         y = dot(silu(v).astype(BF16), w2[...])
         feats_in = ef[rows, :].astype(F32)
         update = feats_in + layer_norm(y, gain, shift)
         live = f * edges + k + iota((step, 1), 0) < count
         oute[rows, :] = jnp.where(live, update, feats_in).astype(BF16)
 
-    messages = oute[...]
-    halo_selT = (iota((listed, edges), 0) + region == row_index).astype(F32).astype(BF16)
-    part[0:listed, :] = dot(halo_selT, messages)
-    pair_out = agg_out
-    pair_out[0:listed, :] = part[0:listed, theirs].astype(BF16)
-    first_pair = pltpu.make_async_remote_copy(
-        pair_out.at[0:listed, :], pair.at[0:listed, :], p_s.at[0], p_r.at[0],
-        device_id=to(g, partner), device_id_type=MESH)
-    first_pair.start()
-    own_selT = (iota((region, edges), 0) == row_index).astype(F32).astype(BF16)
-    part[listed:listed + region, :] = dot(own_selT, messages)
-    pair_out[listed:listed + region, :] = part[listed:listed + region, theirs].astype(BF16)
-    second_pair = pltpu.make_async_remote_copy(
-        pair_out.at[listed:listed + region, :], pair.at[listed:listed + region, :], p_s.at[1], p_r.at[1],
-        device_id=to(g, partner), device_id_type=MESH)
-    second_pair.start()
+    bounds = ((region, region + listed), (0, region))
+    pairs = []
+    for i, (lo, hi) in enumerate(bounds):
+        pair_out[lo:hi, :] = dot(recv_selT[lo:hi, :], oute[:, theirs]).astype(BF16)
+        pairs.append(pltpu.make_async_remote_copy(
+            pair_out.at[lo:hi, :], pair.at[lo:hi, :], p_s.at[i], p_r.at[i],
+            device_id=to(g, partner), device_id_type=MESH))
+        pairs[i].start()
+        if i == 0:
+            part[lo:hi, :] = dot(recv_selT[lo:hi, :], oute[:, mine])
+    first_pair, second_pair = pairs
 
     first_pair.wait_recv()
     for c in halo_copies.values():
         c.wait_send()
-    lst[...] = (part[0:listed, mine] + pair[0:listed, :].astype(F32)).astype(BF16)
+    lst[...] = (part[region:region + listed, :] + pair[region:region + listed, :].astype(F32)).astype(BF16)
     back = {}
     for i in order:
         d, first, rows = blocks[i]
@@ -228,54 +231,45 @@
             device_id=to(lax.rem(g + d, groups), f), device_id_type=MESH)
         back[i].start()
 
+    part[0:region, :] = dot(recv_selT[0:region, :], oute[:, mine])
     for load in loads[10:14]:
         load.wait()
     node_in = nf[...]
     node_pre = dot(node_in, n1[0:width, :])
     second_pair.wait_recv()
-    total = part[listed:listed + region, mine] + pair[listed:listed + region, :].astype(F32)
-    for i in order:
-        d, first, rows = blocks[i]
+    part[0:region, :] += pair[0:region, :].astype(F32)
+    for i in order:
         back[i].wait_recv()
-        total += dot(list_rows(d, rows).astype(BF16), ret[first:first + rows, :])
-    part[0:region, 0:half] = total
-
-    chip_rows = 2 * n_own
-    for j in range(1, chips):
-        at = pl.ds(pl.multiple_of(lax.rem(chip + j, chips) * chip_rows, chip_rows), chip_rows)
-        cross[0, j - 1] = part[at, 0:half].astype(BF16)
+    total = part[0:region, :] + dot(list_selT[...], ret[...])
+    own16[...] = total.astype(BF16)
+    part[0:region, :] = total
+
     crosses = []
-    for j in range(1, chips):
+    for k in range(1, feats):
+        target = lax.rem(f + k, feats)
         crosses.append(pltpu.make_async_remote_copy(
-            cross.at[0, j - 1], cross.at[1, j - 1], x_s.at[j - 1], x_r.at[j - 1],
-            device_id=to(g, lax.rem(chip + j, chips) * 2 + h), device_id_type=MESH))
+            own16.at[pl.ds(pl.multiple_of(target * n_own, n_own), n_own), :], sums.at[k - 1],
+            x_s.at[k - 1], x_r.at[k - 1], device_id=to(g, target), device_id_type=MESH))
         crosses[-1].start()
-
-    def chip_total(which):
-        at = pl.ds(pl.multiple_of((chip * 2 + which) * n_own, n_own), n_own)
-        rows = part[at, 0:half]
-        local = pl.ds(pl.multiple_of(which * n_own, n_own), n_own)
-        for j in range(1, chips):
-            rows = rows + cross[1, j - 1, local, :].astype(F32)
-        return rows.astype(BF16)
-
     for c in crosses:
         c.wait_recv()
-    agg[0, :, 0:half] = chip_total(other)
-    last = pltpu.make_async_remote_copy(
-        agg.at[0, :, 0:half], agg.at[1, :, mine], d_s.at[0], d_r.at[0],
-        device_id=to(g, partner), device_id_type=MESH)
-    last.start()
-    agg[1, :, mine] = chip_total(h)
-    last.wait_recv()
-    node_pre = node_pre + dot(agg[1], n1[width:2 * width, :])
+    kept, given = part[own_rows, :], None
+    for k in range(1, feats):
+        rows = sums[k - 1].astype(F32)
+        if k % 2 == 0:
+            kept = kept + rows
+        else:
+            given = rows if given is None else given + rows
+    first_w = pl.ds(pl.multiple_of(width + h * half, half), half)
+    second_w = pl.ds(pl.multiple_of(width + other * half, half), half)
+    node_pre = node_pre + dot(kept.astype(BF16), n1[first_w, :]) + dot(given.astype(BF16), n1[second_w, :])
     node_out = dot(silu(node_pre).astype(BF16), n2[...])
     outn[...] = (node_in.astype(F32) + layer_norm(node_out, ng[...].astype(F32).reshape(1, width), ns[...].astype(F32).reshape(1, width))).astype(BF16)
 
     own_copy.wait_send()
     for c in chip_copies + relays + list(share.values()) + [first_pair, second_pair]:
         c.wait_send()
-    for c in list(back.values()) + crosses + [last]:
+    for c in list(back.values()) + crosses:
         c.wait_send()
 
 
@@ -308,18 +302,22 @@
             pltpu.VMEM(node_w1.shape, BF16), pltpu.VMEM(node_w2.shape, BF16),
             pltpu.VMEM((region, width), BF16),
             pltpu.VMEM((listed, half), BF16),
-            pltpu.VMEM((listed + region, width), F32),
+            pltpu.VMEM((listed + region, half), F32),
             pltpu.VMEM((listed + region, half), BF16),
             pltpu.VMEM((listed, width), BF16),
             pltpu.VMEM((listed, half), BF16),
             pltpu.VMEM((listed + region, half), BF16),
-            pltpu.VMEM((2, chips - 1, 2 * n_own, half), BF16),
-            pltpu.VMEM((2, n_own, width), BF16),
+            pltpu.VMEM((region, half), BF16),
+            pltpu.VMEM((feats - 1, n_own, half), BF16),
             pltpu.VMEM((edges, edge_w1.shape[1]), F32),
+            pltpu.VMEM((listed, region), BF16),
+            pltpu.VMEM((region, listed), BF16),
+            pltpu.VMEM((edges, region + listed), BF16),
+            pltpu.VMEM((region + listed, edges), BF16),
             dma(14),
             dma(links), dma(links), dma(chips - 1), dma(chips - 1),
             dma(blocks), dma(blocks), dma(blocks), dma(blocks),
-            dma(2), dma(2), dma(blocks), dma(blocks), dma(chips - 1), dma(chips - 1), dma(1), dma(1),
+            dma(2), dma(2), dma(blocks), dma(blocks), dma(feats - 1), dma(feats - 1),
         ],
         compiler_params=pltpu.CompilerParams(
             collective_id=0, has_side_effects=True, vmem_limit_bytes=60 * 1024 * 1024),

time: 36.4 us -> 35.1 us (0.964)
  Pallas kernels: 33.5 us -> 32 us
    pallas_call x1, Pallas kernels: 33.5 us -> 32 us  [per_device(): pl.pallas_call(functools.partial(kernel, groups, feats), out_shape=(pltpu...]
where the time goes in v3:
time: 35.1 us; the launch traced here: 34.8 us
  Pallas kernels  32 us (91%)
  local copies, waits for them, and re-layouts  1.43 us (4%)
  between operations  1.29 us (4%)
    pallas_call x1, Pallas kernels, per_device(): pl.pallas_call(functools.partial(kernel, groups, feats), out_shape=(pltpu...  32 us
    unnamed x2, local copies, waits for them, and re-layouts  1.43 us

profile of v3, /device:TPU:1, one launch (start us, length us, event | category | flops | bytes accessed | tf_op | source)
XLA Modules:
  0.0 34.8 jit_solution(16250898158285412907)
XLA Ops:
  1.3 32.0 %shard_map.149 = (bf16[512,512]{1,0:T(8,128)(2,1)S(1)}, bf16[80,512]{1,0:T(8,128)(2,1)S(1)}) custom-call(s32[1]{0:T(128)S(6)} %copy.20.count_hbm, bf16[80,512]{1,0:T(8,128)(2,1)} %nf_hbm.1, s32[1,512]{1,0:T(1,128)} %bitcast.2, s32[1,512]{1,0:T(1,128)} %bitcast.3, s32[1,8,96]{2,1,0:T(8,128)} %list_hbm.1, bf16[512]{0:T(512)(128)(2,1)} %eg_hbm.1, ...), custom_call_target="tpu_custom_call" | custom-call | tf_op jit(solution)/shard_map/pallas_call | solution.py:292
  33.3 0.8 %copy.18 = bf16[512,512]{1,0:T(8,128)(2,1)} copy(bf16[512,512]{1,0:T(8,128)(2,1)S(1)} %get-tuple-element.2) | data formatting | bytes 1048576
  34.1 0.6 %copy.19 = bf16[80,512]{1,0:T(8,128)(2,1)} copy(bf16[80,512]{1,0:T(8,128)(2,1)S(1)} %get-tuple-element.3) | data formatting | bytes 163840
